TPU v7x, 256 devices: a 8x8x2 block of a 8x8x16 slice. The times are simulated.
256 devices in a mesh: groups: 2 (over z), freq: 128 (over x, y, core).
Axes of the slice: x: 8, y: 8, z: 2, core: 2. Of those that a mesh axis runs over, the one named last changes fastest.
The devices are a block of a 8x8x16 slice.
Arguments:
- traces: bfloat16 [1024, 2048, 256], P('freq', None, 'groups'), parts along dimension 2, may hold values from -24 to 24
- freq_index: int32 [128], replicated, may hold values from 1 to 511
- block_map: int32 [64, 64], replicated, may hold values 0 or 1
- green_rec: bfloat16 [128, 2, 2048, 1536], P('freq', None, None, 'groups'), parts along dimension 3, may hold values from -0.5 to 0.5
- green_src: bfloat16 [128, 2, 128, 1536], P('freq', None, None, 'groups'), parts along dimension 3, may hold values from -0.03125 to 0.03125
Outputs:
- image: float32 [1536], P(('groups', 'freq')), parts along dimension 0
There are 2 independent parts, one for each index of `groups`. A program takes and returns all parts, laid end to end along the dimension named above; an argument that names none is the same for every part. Nothing has to cross between parts.
Inputs may be any that keep to these rules, and one draw needn't show every extreme that they name: `freq_index`: frequency bins; they may repeat. `block_map`: 1 where a receiver block lies in an image tile's aperture.
All inputs are finite; a program needn't handle non-finite values.
Results may differ from a plain program's by a relative error of at most 0.0038.
Values may be sent and summed in bfloat16 or wider, within the bound.
A program may use at most 64 MiB of HBM per device.

v0:
```python
import math

import jax
import jax.numpy as jnp
from jax import lax
from jax.sharding import Mesh
from jax.sharding import PartitionSpec as P

FREQ = ("freq_0", "freq_1", "freq_2")
GROUPS_FREQ = ("groups", "freq_0", "freq_1", "freq_2")


def sum_in_order(parts, axes, order):
    inside = parts.shape[1:]
    parts = parts.reshape(*(lax.axis_size(a) for a in axes), *inside)
    parts = jnp.moveaxis(parts, order, range(len(axes))).reshape(-1, *inside)
    for k in order:
        parts = lax.psum_scatter(parts, axes[k], scatter_dimension=0, tiled=True)
    return parts[0]


def split_up(array, dim, length):
    dims = array.shape
    parts = array.reshape(*dims[:dim], length, dims[dim] // length, *dims[dim + 1 :])
    return jnp.moveaxis(parts, dim, 0)


def scatter_axes(array, axes, order, dim):
    length = lax.axis_size(axes)
    return sum_in_order(split_up(array, dim, length), axes, order)


def dft_table(freq_index, length):
    sample_index = jnp.arange(length, dtype=jnp.int32)
    phases = freq_index[:, None] * sample_index[None, :] % length
    angles = phases.astype(jnp.float32) * jnp.float32(2.0 * math.pi / length)
    stacked = jnp.stack((jnp.cos(angles), -jnp.sin(angles)), axis=1)
    return stacked.reshape(freq_index.shape[0] * 2, length).astype(jnp.bfloat16)


def expand_map(block_map, receivers, points):
    row_span = receivers // block_map.shape[0]
    col_span = points // block_map.shape[1]
    return jnp.repeat(jnp.repeat(block_map, row_span, axis=0), col_span, axis=1).astype(
        jnp.bfloat16
    )


def transform(cos_table, records, length):
    spectrum = jnp.dot(cos_table, records.reshape(length, -1), preferred_element_type=jnp.float32)
    return (spectrum * (1.0 / math.sqrt(length))).astype(jnp.bfloat16)


def back_project(spectra, masked):
    swapped = jnp.stack((spectra[:, 1], -spectra[:, 0]), axis=1)
    blocks = jnp.stack((spectra, swapped), axis=1)
    return jnp.einsum("fcrx,focrs->fosx", masked, blocks, preferred_element_type=jnp.float32)


def body(traces, freq_index, block_map, green_rec, green_src):
    shards = lax.axis_size(FREQ)
    length = traces.shape[0] * shards
    receivers = traces.shape[1]
    shots = traces.shape[2]
    freqs = freq_index.shape[0]
    cos_table = dft_table(freq_index, length)
    masked = green_rec * expand_map(block_map, receivers, green_rec.shape[3])[None, None]
    regrouped = lax.all_to_all(traces, FREQ, split_axis=2, concat_axis=0, tiled=True)
    spectrum = transform(cos_table, regrouped, length).reshape(freqs, 2, receivers, shots // shards)
    gathered = lax.all_to_all(spectrum, FREQ, split_axis=0, concat_axis=3, tiled=True)
    back_field = back_project(gathered, masked)
    partial_image = jnp.sum(green_src.astype(jnp.float32) * back_field, axis=(0, 1, 2))
    return scatter_axes(partial_image, FREQ, (2, 0, 1), 0)


def solution(mesh):
    split = Mesh(
        mesh.devices.reshape(mesh.shape["groups"], 8, 8, 2),
        ("groups", "freq_0", "freq_1", "freq_2"),
    )
    placed = (
        P(FREQ, None, "groups"),
        P(),
        P(),
        P(FREQ, None, None, "groups"),
        P(FREQ, None, None, "groups"),
    )
    return jax.shard_map(
        body, mesh=split, in_specs=placed, out_specs=P(GROUPS_FREQ), check_vma=False
    )
```

profile of v0, /device:TPU:514, one launch (start us, length us, event | category | flops | bytes accessed | tf_op | source)
XLA Modules:
  0.0 261.6 jit_solution(12877544963939775188)
XLA Ops:
  6.5 6.7 %copy.34 = bf16[8,2048,128]{1,0,2:T(8,128)(2,1)} copy(bf16[8,2048,128]{2,1,0:T(8,128)(2,1)} %param.5) | data formatting | bytes 8388608 | tf_op args[0]
  13.2 27.6 %all-to-all-start = ((bf16[8,2048,128]{1,0,2:T(8,128)(2,1)}), bf16[8,2048,128]{1,0,2:T(8,128)(2,1)}, u32[]{:S(2)}, u32[]{:S(2)}) async-start(bf16[8,2048,128]{1,0,2:T(8,128)(2,1)} %copy.34), calls=%async_computation | async-start | bytes 8388608 | tf_op jit(solution)/shard_map/all_to_all | solution.py:68
  40.8 2.4 cosine_convert_fusion
  43.4 0.5 copy.33
  43.9 0.2 convert_element_type.47
  44.1 92.4 %all-to-all-done = bf16[8,2048,128]{1,0,2:T(8,128)(2,1)} async-done(((bf16[8,2048,128]{1,0,2:T(8,128)(2,1)}), bf16[8,2048,128]{1,0,2:T(8,128)(2,1)}, u32[]{:S(2)}, u32[]{:S(2)}) %all-to-all-start) | async-done | bytes 4194336 | tf_op jit(solution)/shard_map/all_to_all | solution.py:68
  136.5 3.4 %fusion.9 = bf16[256,2048]{1,0:T(8,128)(2,1)S(1)} fusion(bf16[256,1024]{1,0:T(8,128)(2,1)S(1)} %convert_element_type.47, bf16[8,2048,128]{1,0,2:T(8,128)(2,1)} %all-to-all-done), kind=kOutput, calls=%fused_computation.7 | convolution fusion | flops 1074790400 | bytes 5767168 | tf_op jit(solution)/shard_map/dot_general | solution.py:50
  139.9 1.5 reshape.135
  141.4 16.6 %all-to-all-start.1 = ((bf16[128,2,2048,1]{2,1,3,0:T(2,128)(2,1)}), bf16[128,2,2048,1]{2,1,3,0:T(2,128)(2,1)}, u32[]{:S(2)}, u32[]{:S(2)}) async-start(bf16[128,2,2048,1]{2,1,3,0:T(2,128)(2,1)} %bitcast.3), calls=%async_computation.1 | async-start | bytes 2097152 | tf_op jit(solution)/shard_map/all_to_all | solution.py:70
  158.1 0.2 reduce-scatter.6.cloned.1.call-start
  158.7 2.5 broadcast_in_dim.10
  161.1 4.7 %convert_element_type.51 = bf16[2048,768]{0,1:T(8,128)(2,1)S(1)} reshape(bf16[2048,64,12]{0,2,1:T(8,128)(2,1)} %broadcast_in_dim.10) | data formatting | bytes 6291456 | tf_op jit(solution)/shard_map/convert_element_type | solution.py:44
  165.8 2.8 %copy.38 = bf16[2048,768]{1,0:T(8,128)(2,1)} copy(bf16[2048,768]{0,1:T(8,128)(2,1)S(1)} %convert_element_type.51) | data formatting | bytes 6291456 | tf_op jit(solution)/shard_map/convert_element_type | solution.py:44
  168.7 19.9 %all-to-all-done.1 = bf16[128,2,2048,1]{2,1,3,0:T(2,128)(2,1)} async-done(((bf16[128,2,2048,1]{2,1,3,0:T(2,128)(2,1)}), bf16[128,2,2048,1]{2,1,3,0:T(2,128)(2,1)}, u32[]{:S(2)}, u32[]{:S(2)}) %all-to-all-start.1) | async-done | bytes 1048608 | tf_op jit(solution)/shard_map/all_to_all | solution.py:70
  188.6 1.6 copy.51
  190.4 4.7 %fusion.20 = f32[768]{0:T(1024)S(1)} fusion(bf16[1,2,2048,768]{3,2,1,0:T(8,128)(2,1)} %param.8, bf16[2048,768]{1,0:T(8,128)(2,1)S(1)} %copy-done, bf16[1,1,2,2048,128]{3,4,2,1,0:T(8,128)(2,1)S(1)} %maximum_bitcast_fusion.8, bf16[1,1,2,2048,128]{3,4,2,1,0:T(8,128)(2,1)S(1)} %bitcast.65, bf16[1,2,128,768]{3,2,1,0:T(8,128)(2,1)S(1)} %copy-done.3), kind=kOutput, calls=%fused_computation.13 | convolution fusion | flops 1615396096 | bytes 11930624 | tf_op jit(solution)/shard_map/fcrx,focrs->fosx/dot_general | solution.py:57
  195.3 0.6 copy.47
  196.0 0.6 dynamic-slice
  196.6 0.7 dynamic-slice.2
  197.9 21.5 %reduce-scatter.6.cloned.1.call-done = f32[64,6]{1,0:T(8,128)} async-done(((f32[128,6]{1,0:T(8,128)}), f32[64,6]{1,0:T(8,128)}) %reduce-scatter.6.cloned.1.call-update) | async-done | bytes 1552
  219.4 0.8 copy.42
  220.2 15.7 %all-reduce = f32[64,6]{0,1:T(8,128)S(1)} all-reduce(f32[64,6]{0,1:T(8,128)S(1)} %copy.42), channel_id=3, replica_groups=mesh['groups'=2,'freq_0'=8,'freq_1'=8,'freq_2'=2] {'freq_0'}, use_global_device_ids=true, to_apply=%region_2.3.clone | all-reduce | flops 384 | bytes 3072
  235.9 17.4 %all-reduce.1 = f32[8,6]{0,1:T(8,128)S(1)} all-reduce(f32[8,6]{0,1:T(8,128)S(1)} %constant_dynamic-slice_fusion), channel_id=4, replica_groups=mesh['groups'=2,'freq_0'=8,'freq_1'=8,'freq_2'=2] {'freq_1'}, use_global_device_ids=true, to_apply=%region_3.4.clone | all-reduce | flops 48 | bytes 384
  253.3 1.4 dynamic-slice_reduce_fusion
  (21 shorter events, 0.8 us)
Async XLA Ops:
  13.2 27.6 %copy-start.2 = (s32[128]{0:T(128)S(1)}, s32[128]{0:T(128)}, u32[]{:S(2)}) copy-start(s32[128]{0:T(128)} %param.6) | copy-start | bytes 1540
  13.2 123.2 %all-to-all-start = ((bf16[8,2048,128]{1,0,2:T(8,128)(2,1)}), bf16[8,2048,128]{1,0,2:T(8,128)(2,1)}, u32[]{:S(2)}, u32[]{:S(2)}) async-start(bf16[8,2048,128]{1,0,2:T(8,128)(2,1)} %copy.34), calls=%async_computation | async-start | bytes 8388608 | tf_op jit(solution)/shard_map/all_to_all | solution.py:68
  44.1 114.2 %copy-start.1 = (s32[64,64]{1,0:T(8,128)S(1)}, s32[64,64]{1,0:T(8,128)}, u32[]{:S(2)}) copy-start(s32[64,64]{1,0:T(8,128)} %param.7) | copy-start | bytes 49156
  141.4 47.2 %all-to-all-start.1 = ((bf16[128,2,2048,1]{2,1,3,0:T(2,128)(2,1)}), bf16[128,2,2048,1]{2,1,3,0:T(2,128)(2,1)}, u32[]{:S(2)}, u32[]{:S(2)}) async-start(bf16[128,2,2048,1]{2,1,3,0:T(2,128)(2,1)} %bitcast.3), calls=%async_computation.1 | async-start | bytes 2097152 | tf_op jit(solution)/shard_map/all_to_all | solution.py:70
  158.1 61.3 %reduce-scatter.6.cloned.1.call-start = ((), (), s32[]{:S(2)}) async-start(), calls=%async_computation.3 | async-start | bytes 98304
  168.7 21.7 %copy-start = (bf16[2048,768]{1,0:T(8,128)(2,1)S(1)}, bf16[2048,768]{1,0:T(8,128)(2,1)}, u32[]{:S(2)}) copy-start(bf16[2048,768]{1,0:T(8,128)(2,1)} %copy.38) | copy-start | bytes 9437188
  168.7 21.7 %copy-start.3 = (bf16[1,2,128,768]{3,2,1,0:T(8,128)(2,1)S(1)}, bf16[1,2,128,768]{3,2,1,0:T(8,128)(2,1)}, u32[]{:S(2)}) copy-start(bf16[1,2,128,768]{3,2,1,0:T(8,128)(2,1)} %param.9) | copy-start | bytes 1179652
  190.4 5.6 %copy-start.5 = (u32[256]{0:T(256)S(1)}, u32[256]{0:T(256)}, u32[]{:S(2)}) copy-start(u32[256]{0:T(256)} %constant.26) | copy-start | bytes 3076
  190.4 6.2 %copy-start.4 = (u32[256]{0:T(256)S(1)}, u32[256]{0:T(256)}, u32[]{:S(2)}) copy-start(u32[256]{0:T(256)} %constant.30) | copy-start | bytes 3076
Sparse Core Ops, SparseCore 0:
  196.1 23.2 reduce-scatter.5
where the time goes:
time: 262 us
  waiting for transfers between devices  134 us (51%)
  starting transfers between devices  44.5 us (17%)
  blocking collectives  33 us (13%)
  local copies, waits for them, and re-layouts  25.1 us (10%)
  between operations  14.3 us (5%)
  matrix products  8.12 us (3%)
  other arithmetic  2.67 us (1%)
    all_to_all x1, waiting for transfers between devices, body(): lax.all_to_all(traces, FREQ, split_axis=2, concat_axis=0, tiled=True)  92.4 us
    unnamed x2, blocking collectives  33 us
    all_to_all x1, starting transfers between devices, body(): lax.all_to_all(traces, FREQ, split_axis=2, concat_axis=0, tiled=True)  27.6 us
    unnamed x2, waiting for transfers between devices  21.5 us
    all_to_all x1, waiting for transfers between devices, body(): lax.all_to_all(spectrum, FREQ, split_axis=0, concat_axis=3, tiled=True)  19.9 us
    all_to_all x1, starting transfers between devices, body(): lax.all_to_all(spectrum, FREQ, split_axis=0, concat_axis=3, tiled=True)  16.6 us
    unnamed x18, local copies, waits for them, and re-layouts  9.5 us
    convert_element_type x3, local copies, waits for them, and re-layouts, expand_map(): jnp.repeat(jnp.repeat(block_map, row_span, axis=0), col_span, axis=1)  7.73 us
  transfers between devices with their start and end apart: 3, of which 3 were waited for; matrix products, arithmetic and copies ran while one was open for 6% of the time, Pallas kernels for 0%

commit v1 on v0

v1 whole, which is shorter than its diff:
```python
import functools
import math

import jax
import jax.numpy as jnp
from jax import lax
from jax.experimental import pallas as pl
from jax.experimental.pallas import tpu as pltpu
from jax.sharding import PartitionSpec as P

MESH = pl.DeviceIdType.MESH
BF16, F32 = jnp.bfloat16, jnp.float32
CHUNKS = 2
SUB = 8
LANES = 128


def dft_table(freq_index, length):
    sample_index = jnp.arange(length, dtype=jnp.int32)
    phases = freq_index[:, None] * sample_index[None, :] % length
    angles = phases.astype(jnp.float32) * jnp.float32(2.0 * math.pi / length)
    stacked = jnp.stack((jnp.cos(angles), -jnp.sin(angles)), axis=1)
    return stacked.reshape(freq_index.shape[0] * 2, length).astype(jnp.bfloat16)


def iota(shape, dim):
    return lax.broadcasted_iota(jnp.int32, shape, dim)


def one_hot(pred):
    return jnp.where(pred, 1.0, 0.0).astype(F32)


def swap_matrix(outer, inner):
    size = outer * inner
    row, col = iota((size, size), 0), iota((size, size), 1)
    return one_hot((row // outer == col % inner) & (row % outer == col // inner)).astype(BF16)


def exact_dot(a, b):
    return jnp.dot(a, b, preferred_element_type=F32, precision=lax.Precision.HIGHEST)


def kernel(
    n, traces, table, block_map, green_rec, green_src, out,
    xbuf, xt, yb, spec, pbuf, masked, colmask, src, back, istage, ibuf,
    x_send, x_recv, p_send, p_recv, i_send, i_recv, g_sem, s_sem,
):
    me = lax.axis_index("freq")
    tsub = traces.shape[0]
    length = n * tsub
    receivers = traces.shape[1]
    points = green_rec.shape[2]
    per_chunk = receivers // CHUNKS

    def peer(d):
        return lax.rem(me + d, n)

    load_rec = pltpu.make_async_copy(green_rec, masked, g_sem)
    load_src = pltpu.make_async_copy(green_src, src, s_sem)
    load_rec.start()
    load_src.start()

    barrier = pltpu.get_barrier_semaphore()

    @pl.loop(1, n)
    def _(d):
        pl.semaphore_signal(barrier, inc=1, device_id={"freq": peer(d)}, device_id_type=MESH)

    pl.semaphore_wait(barrier, n - 1)

    for c in range(CHUNKS):
        def block_of(j, c=c):
            start = pl.multiple_of(c * per_chunk + j * SUB, SUB)
            return traces.at[:, pl.ds(start, SUB), :]

        @pl.loop(1, n)
        def _(d, c=c, block_of=block_of):
            j = peer(d)
            pltpu.make_async_remote_copy(
                src_ref=block_of(j), dst_ref=xbuf.at[c, me],
                send_sem=x_send, recv_sem=x_recv.at[c],
                device_id={"freq": j}, device_id_type=MESH,
            ).start()

        pltpu.make_async_copy(block_of(me), xbuf.at[c, me], x_recv.at[c]).start()

    tiles = block_map.shape[1]
    rblk = block_map.shape[0]
    spread = one_hot(iota((tiles, points), 1) // (points // tiles) == iota((tiles, points), 0))
    colmask[...] = jnp.dot(block_map[...].astype(F32), spread, preferred_element_type=F32)
    load_rec.wait()
    load_src.wait()
    span = receivers // rblk

    @pl.loop(0, rblk)
    def _(b):
        row = jnp.broadcast_to(colmask[pl.ds(b, 1), :], (span, points)).astype(BF16)
        rows = pl.ds(pl.multiple_of(b * span, span), span)
        for c in range(2):
            masked[c, rows, :] = masked[c, rows, :] * row

    back[...] = jnp.zeros_like(back)
    tb = 256 // SUB
    kb = tb // tsub
    swap_in = swap_matrix(tb, SUB)
    swap_out = swap_matrix(SUB, tb)
    fcs = table.shape[0]
    scale = 1.0 / math.sqrt(length)

    def transform(c):
        pltpu.make_async_copy(xbuf.at[c], xbuf.at[c], x_recv.at[c]).wait()

        @pl.loop(0, length // tb // 2)
        def _(b):
            both = [
                xbuf[c, pl.ds((2 * b + h) * kb, kb)].reshape(tb * SUB, LANES) for h in range(2)
            ]
            y = jnp.dot(swap_in, jnp.concatenate(both, axis=1), preferred_element_type=F32)
            y = y.astype(BF16).reshape(SUB, tb, 2 * LANES)
            for h in range(2):
                rows = pl.ds(pl.multiple_of((2 * b + h) * tb, tb), tb)
                for r in range(SUB):
                    xt[r // 2, rows, (r % 2) * LANES : (r % 2 + 1) * LANES] = y[
                        r, :, h * LANES : (h + 1) * LANES
                    ]

        for rp in range(SUB // 2):
            o = jnp.dot(table[...], xt[rp], preferred_element_type=F32) * scale
            o = o.astype(BF16)
            yb[2 * rp] = o[:, :LANES]
            yb[2 * rp + 1] = o[:, LANES:]

        for j in range(0, fcs // tb, 2):
            both = [yb[:, (j + h) * tb : (j + h + 1) * tb, :].reshape(256, LANES) for h in range(2)]
            y = jnp.dot(swap_out, jnp.concatenate(both, axis=1), preferred_element_type=F32)
            y = y.astype(BF16)
            for h in range(2):
                spec[c, (j + h) * tb // 2 : (j + h + 1) * tb // 2] = y[
                    :, h * LANES : (h + 1) * LANES
                ].reshape(tb // 2, 2, SUB, LANES)

        @pl.loop(1, n)
        def _(d):
            j = peer(d)
            pltpu.make_async_remote_copy(
                src_ref=spec.at[c, j], dst_ref=pbuf.at[c, me],
                send_sem=p_send, recv_sem=p_recv.at[c],
                device_id={"freq": j}, device_id_type=MESH,
            ).start()

        pbuf[c, me] = spec[c, me]

    def project(c):
        most = pbuf.at[c, pl.ds(0, n - 1)]
        pltpu.make_async_copy(most, most, p_recv.at[c]).wait()
        rows = slice(c * per_chunk, (c + 1) * per_chunk)
        p0 = pbuf[c, :, 0].reshape(per_chunk, LANES)
        p1 = pbuf[c, :, 1].reshape(per_chunk, LANES)
        dims = (((0,), (0,)), ((), ()))
        back[...] += lax.dot_general(
            jnp.concatenate([p0, p1], axis=1), masked[0, rows, :], dims, preferred_element_type=F32
        )
        back[...] += lax.dot_general(
            jnp.concatenate([p1, -p0], axis=1), masked[1, rows, :], dims, preferred_element_type=F32
        )

    for c in range(CHUNKS):
        transform(c)
        if c > 0:
            project(c - 1)
    project(CHUNKS - 1)

    shots = src.shape[1]
    image = jnp.zeros((1, points), F32)
    for o in range(2):
        image += jnp.sum(
            src[o].astype(F32) * back[o * shots : (o + 1) * shots, :], axis=0, keepdims=True
        )
    each = points // n
    mine = one_hot(iota((n, points), 1) // each == iota((n, points), 0)) * image
    fold = one_hot(iota((points, LANES), 0) % each == iota((points, LANES), 1))
    istage[...] = exact_dot(mine, fold).reshape(n, 1, LANES)

    @pl.loop(1, n)
    def _(d):
        j = peer(d)
        pltpu.make_async_remote_copy(
            src_ref=istage.at[j], dst_ref=ibuf.at[me],
            send_sem=i_send, recv_sem=i_recv,
            device_id={"freq": j}, device_id_type=MESH,
        ).start()

    ibuf[me] = istage[me]
    most = ibuf.at[pl.ds(0, n - 1)]
    pltpu.make_async_copy(most, most, i_recv).wait()
    out[...] = jnp.sum(ibuf[...], axis=0)

    for c in range(CHUNKS):
        most = xbuf.at[c, pl.ds(0, n - 1)]
        pltpu.make_async_copy(most, most, x_send).wait()
        most = pbuf.at[c, pl.ds(0, n - 1)]
        pltpu.make_async_copy(most, most, p_send).wait()
    most = ibuf.at[pl.ds(0, n - 1)]
    pltpu.make_async_copy(most, most, i_send).wait()


def body(traces, freq_index, block_map, green_rec, green_src):
    n = lax.axis_size("freq")
    tsub, receivers, shots = traces.shape
    length = tsub * n
    points = green_rec.shape[3]
    fcs = 2 * freq_index.shape[0]
    table = dft_table(freq_index, length)
    per = receivers // CHUNKS
    assert freq_index.shape[0] == n and per == n * SUB and shots == LANES
    any_spec = pl.BlockSpec(memory_space=pl.ANY)
    vmem = pl.BlockSpec(memory_space=pltpu.VMEM)
    dma = pltpu.SemaphoreType.DMA
    out = pl.pallas_call(
        functools.partial(kernel, n),
        out_shape=jax.ShapeDtypeStruct((1, LANES), F32),
        in_specs=[any_spec, vmem, vmem, any_spec, any_spec],
        out_specs=vmem,
        scratch_shapes=[
            pltpu.VMEM((CHUNKS, n, tsub, SUB, LANES), BF16),
            pltpu.VMEM((SUB // 2, length, 2 * LANES), BF16),
            pltpu.VMEM((SUB, fcs, LANES), BF16),
            pltpu.VMEM((CHUNKS, n, 2, SUB, LANES), BF16),
            pltpu.VMEM((CHUNKS, n, 2, SUB, LANES), BF16),
            pltpu.VMEM((2, receivers, points), BF16),
            pltpu.VMEM((block_map.shape[0], points), F32),
            pltpu.VMEM((2, shots, points), BF16),
            pltpu.VMEM((2 * shots, points), F32),
            pltpu.VMEM((n, 1, LANES), F32),
            pltpu.VMEM((n, 1, LANES), F32),
            dma, dma((CHUNKS,)), dma, dma((CHUNKS,)), dma, dma, dma, dma,
        ],
        compiler_params=pltpu.CompilerParams(
            collective_id=0, has_side_effects=True, vmem_limit_bytes=60 * 2**20
        ),
    )(traces, table, block_map, green_rec[0], green_src[0])
    return out[0, : points // n]


def solution(mesh):
    placed = (
        P("freq", None, "groups"),
        P(),
        P(),
        P("freq", None, None, "groups"),
        P("freq", None, None, "groups"),
    )
    return jax.shard_map(
        body, mesh=mesh, in_specs=placed, out_specs=P(("groups", "freq")), check_vma=False
    )
```

time: 262 us -> 210 us (0.80)
  Pallas kernels: 0 us -> 201 us
  waiting for transfers between devices: 134 us -> 0 us
  starting transfers between devices: 44.5 us -> 0 us
  blocking collectives: 33 us -> 0 us
  local copies, waits for them, and re-layouts: 25.1 us -> 2.63 us
  between operations: 14.3 us -> 0.03 us
  matrix products: 8.12 us -> 0 us
    pallas_call x0 -> x1, Pallas kernels: none -> 201 us  [body(): pl.pallas_call(functools.partial(kernel, n), out_shape=jax.ShapeDtypeStru...]
    all_to_all x2 -> x0, waiting for transfers between devices: 112 us -> none  [the longest x1 92.4 us: body(): lax.all_to_all(traces, FREQ, split_axis=2, concat_axis=0, tiled=True)]
    all_to_all x2 -> x0, starting transfers between devices: 44.2 us -> none  [the longest x1 27.6 us: body(): lax.all_to_all(traces, FREQ, split_axis=2, concat_axis=0, tiled=True)]
    unnamed x2 -> x0, blocking collectives: 33 us -> none
    unnamed x2 -> x0, waiting for transfers between devices: 21.5 us -> none
    unnamed x18 -> x0, local copies, waits for them, and re-layouts: 9.5 us -> none
    dot_general x2 -> x0, matrix products: 8.12 us -> none  [the longest x1 4.68 us: back_project(): jnp.einsum('fcrx,focrs->fosx', masked, blocks, preferred_element_type=jnp...]
    convert_element_type x3 -> x0, local copies, waits for them, and re-layouts: 7.73 us -> none  [expand_map(): jnp.repeat(jnp.repeat(block_map, row_span, axis=0), col_span, axis=1)]
  transfers between devices with their start and end apart: 3 -> 0, of which waited for: 3 -> 0; matrix products, arithmetic and copies ran while one was open for 6% -> 0% of each run, Pallas kernels for 0% -> 0%
where the time goes in v1:
time: 210 us; the launch traced here: 207 us
  Pallas kernels  201 us (96%)
  other arithmetic  3.16 us (2%)
  local copies, waits for them, and re-layouts  2.63 us (1%)
    pallas_call x1, Pallas kernels, body(): pl.pallas_call(functools.partial(kernel, n), out_shape=jax.ShapeDtypeStru...  201 us

profile of v1, /device:TPU:514, one launch (start us, length us, event | category | flops | bytes accessed | tf_op | source)
XLA Modules:
  0.0 207.2 jit_solution(12661149560537897410)
XLA Ops:
  0.0 3.1 %cosine_convert_fusion = (bf16[128,1,1024]{2,0,1:T(8,128)(2,1)S(1)}, bf16[128,1,1024]{2,0,1:T(8,128)(2,1)S(1)}) fusion(s32[128]{0:T(128)} %param.6), kind=kLoop, calls=%fused_computation.8 | loop fusion | flops 2228224 | bytes 524800 | tf_op jit(solution)/shard_map/convert
  3.1 0.1 pad_maximum_fusion
  3.2 0.5 copy.6
  3.7 1.0 convert_element_type.18.table
  4.7 201.4 %shard_map.55 = f32[1,128]{1,0:T(1,128)} custom-call(bf16[8,2048,128]{2,1,0:T(8,128)(2,1)} %traces.1, bf16[256,1024]{1,0:T(8,128)(2,1)} %convert_element_type.18.table, s32[64,64]{1,0:T(8,128)} %block_map.1, bf16[2,2048,768]{2,1,0:T(8,128)(2,1)} %bitcast.4, bf16[2,128,768]{2,1,0:T(8,128)(2,1)} %bitcast.5), custom_call_target="tpu_custom_call" | custom-call | tf_op jit(solution)/shard_map/pallas_call | solution.py:220
  206.1 1.1 slice_bitcast_fusion

commit v2 on v0

v2 whole, which is shorter than its diff:
```python
import functools
import math

import jax
import jax.numpy as jnp
from jax import lax
from jax.experimental import pallas as pl
from jax.experimental.pallas import tpu as pltpu
from jax.sharding import PartitionSpec as P

MESH = pl.DeviceIdType.MESH
BF16, F32 = jnp.bfloat16, jnp.float32
CHUNKS = 2
SUB = 8
LANES = 128
SIDE, CORES = 8, 2
ORBITS = (SIDE // 2) ** 2 - 1
STRIDE, FIRST = 11, 3
BLOCK = 256
UNROLL = 3


def iota(shape, dim):
    return lax.broadcasted_iota(jnp.int32, shape, dim)


def one_hot(pred):
    return jnp.where(pred, 1.0, 0.0).astype(F32)


def permutation(size, source):
    row, col = iota((size, size), 0), iota((size, size), 1)
    return one_hot(source(row) == col).astype(BF16)


def turned(dx, dy, times):
    for _ in range(times):
        dx, dy = -dy, dx
    return dx, dy


def each_peer(me, send):
    core, y, x = me & (CORES - 1), (me // CORES) & (SIDE - 1), me // (CORES * SIDE)

    def at(dx, dy, dc):
        chip = ((x + dx) & (SIDE - 1)) * SIDE + ((y + dy) & (SIDE - 1))
        return chip * CORES + ((core + dc) & (CORES - 1))

    half = SIDE // 2

    @pl.loop(0, ORBITS * CORES, unroll=UNROLL)
    def _(i):
        e = (i * STRIDE + FIRST) % (ORBITS * CORES)
        k, dc = e // CORES, e & (CORES - 1)
        a, b = 1 + (k & (half - 1)), (k // half + 1) & (half - 1)
        for times in range(4):
            dx, dy = turned(a, b, times)
            send(at(dx, dy, dc))

    for dx, dy in ((half, 0), (0, half), (half, half)):
        for dc in range(CORES):
            send(at(dx, dy, dc))
    for dc in range(1, CORES):
        send(at(0, 0, dc))


def exact_dot(a, b):
    return jnp.dot(a, b, preferred_element_type=F32, precision=lax.Precision.HIGHEST)


def kernel(
    n, traces, freq_index, block_map, green_rec, green_src, out,
    table, xbuf, xt, yb, spec, pbuf, masked, colmask, src, back, istage, ibuf,
    x_send, x_recv, p_send, p_recv, i_send, i_recv, g_sem, s_sem,
):
    me = lax.axis_index("freq")
    tsub, receivers, _ = traces.shape
    length = n * tsub
    points = green_rec.shape[2]
    per_chunk = receivers // CHUNKS

    barrier = pltpu.get_barrier_semaphore()

    def greet(j):
        pl.semaphore_signal(barrier, inc=1, device_id={"freq": j}, device_id_type=MESH)

    each_peer(me, greet)

    load_rec = pltpu.make_async_copy(green_rec, masked, g_sem)
    load_src = pltpu.make_async_copy(green_src, src, s_sem)

    def block_of(c, j):
        start = pl.multiple_of(c * per_chunk + j * SUB, SUB)
        return traces.at[:, pl.ds(start, SUB), :]

    own = [
        pltpu.make_async_copy(block_of(c, me), xbuf.at[c, me], x_recv.at[c]) for c in range(CHUNKS)
    ]
    for copy in [*own, load_rec, load_src]:
        copy.start()

    with jax.named_scope("barrier"):
        pl.semaphore_wait(barrier, n - 1)

    with jax.named_scope("send"):
        for c in range(CHUNKS):
            def send_block(j, c=c):
                pltpu.make_async_remote_copy(
                    src_ref=block_of(c, j), dst_ref=xbuf.at[c, me],
                    send_sem=x_send, recv_sem=x_recv.at[c],
                    device_id={"freq": j}, device_id_type=MESH,
                ).start()

            each_peer(me, send_block)

    with jax.named_scope("table"):
        freqs = freq_index.shape[1]
        diagonal = iota((freqs, freqs), 0) == iota((freqs, freqs), 1)
        column = jnp.sum(
            jnp.where(diagonal, freq_index[...].astype(F32), 0.0), axis=1, keepdims=True
        ).astype(jnp.int32)
        phases = lax.rem(column * iota((freqs, length), 1), length)
        angles = phases.astype(F32) * jnp.float32(2.0 * math.pi / length)
        table[:freqs] = jnp.cos(angles).astype(BF16)
        table[freqs:] = (-jnp.sin(angles)).astype(BF16)

    with jax.named_scope("mask"):
        rblk, tiles = block_map.shape
        spread = one_hot(iota((tiles, points), 1) // (points // tiles) == iota((tiles, points), 0))
        colmask[...] = jnp.dot(block_map[...].astype(F32), spread, preferred_element_type=F32)
        load_rec.wait()
        load_src.wait()
        span = receivers // rblk

        @pl.loop(0, rblk, unroll=2)
        def _(b):
            row = jnp.broadcast_to(colmask[pl.ds(b, 1), :], (span, points)).astype(BF16)
            rows = pl.ds(pl.multiple_of(b * span, span), span)
            for c in range(2):
                masked[c, rows, :] = masked[c, rows, :] * row

    tb = BLOCK // SUB
    fb = tb // 2
    kb = tb // tsub
    swap_in = permutation(BLOCK, lambda row: row % tb * SUB + row // tb)
    swap_out = permutation(
        BLOCK, lambda row: row % SUB * tb + row // SUB % 2 * fb + row // (2 * SUB)
    )
    scale = 1.0 / math.sqrt(length)
    back[...] = jnp.zeros_like(back)

    def transform(c):
        with jax.named_scope(f"wait_x{c}"):
            pltpu.make_async_copy(xbuf.at[c], xbuf.at[c], x_recv.at[c]).wait()

        with jax.named_scope(f"swap_in{c}"):
            @pl.loop(0, length // tb // 2, unroll=4)
            def _(b):
                both = [
                    xbuf[c, pl.ds((2 * b + h) * kb, kb)].reshape(BLOCK, LANES) for h in range(2)
                ]
                y = jnp.dot(swap_in, jnp.concatenate(both, axis=1), preferred_element_type=F32)
                y = y.astype(BF16).reshape(SUB, tb, 2 * LANES)
                for h in range(2):
                    rows = pl.ds(pl.multiple_of((2 * b + h) * tb, tb), tb)
                    for r in range(SUB):
                        xt[r // 2, rows, (r % 2) * LANES : (r % 2 + 1) * LANES] = y[
                            r, :, h * LANES : (h + 1) * LANES
                        ]

        with jax.named_scope(f"dft{c}"):
            for rp in range(SUB // 2):
                o = jnp.dot(table[...], xt[rp], preferred_element_type=F32) * scale
                o = o.astype(BF16)
                yb[2 * rp] = o[:, :LANES]
                yb[2 * rp + 1] = o[:, LANES:]

        with jax.named_scope(f"swap_out{c}"):
            def gathered(f0):
                parts = [yb[:, p * freqs + f0 : p * freqs + f0 + fb, :] for p in range(2)]
                return jnp.concatenate(parts, axis=1).reshape(BLOCK, LANES)

            for f0 in range(0, freqs, 2 * fb):
                both = [gathered(f0 + h * fb) for h in range(2)]
                y = jnp.dot(swap_out, jnp.concatenate(both, axis=1), preferred_element_type=F32)
                y = y.astype(BF16)
                for h in range(2):
                    spec[c, f0 + h * fb : f0 + (h + 1) * fb] = y[
                        :, h * LANES : (h + 1) * LANES
                    ].reshape(fb, 2, SUB, LANES)

        with jax.named_scope(f"scatter{c}"):
            def send_spectrum(j):
                pltpu.make_async_remote_copy(
                    src_ref=spec.at[c, j], dst_ref=pbuf.at[c, me],
                    send_sem=p_send, recv_sem=p_recv.at[c],
                    device_id={"freq": j}, device_id_type=MESH,
                ).start()

            each_peer(me, send_spectrum)
            pbuf[c, me] = spec[c, me]

    def project(c):
        with jax.named_scope(f"wait_p{c}"):
            most = pbuf.at[c, pl.ds(0, n - 1)]
            pltpu.make_async_copy(most, most, p_recv.at[c]).wait()
        with jax.named_scope(f"project{c}"):
            rows = slice(c * per_chunk, (c + 1) * per_chunk)
            p0 = pbuf[c, :, 0].reshape(per_chunk, LANES)
            p1 = pbuf[c, :, 1].reshape(per_chunk, LANES)
            dims = (((0,), (0,)), ((), ()))
            back[...] += lax.dot_general(
                jnp.concatenate([p0, p1], axis=1), masked[0, rows, :], dims,
                preferred_element_type=F32,
            )
            back[...] += lax.dot_general(
                jnp.concatenate([p1, -p0], axis=1), masked[1, rows, :], dims,
                preferred_element_type=F32,
            )

    for c in range(CHUNKS):
        transform(c)
        if c > 0:
            project(c - 1)
    project(CHUNKS - 1)

    with jax.named_scope("image"):
        shots = src.shape[1]
        image = jnp.zeros((1, points), F32)
        for o in range(2):
            image += jnp.sum(
                src[o].astype(F32) * back[o * shots : (o + 1) * shots, :], axis=0, keepdims=True
            )
        each = points // n
        mine = one_hot(iota((n, points), 1) // each == iota((n, points), 0)) * image
        fold = one_hot(iota((points, LANES), 0) % each == iota((points, LANES), 1))
        istage[...] = exact_dot(mine, fold).reshape(n, 1, LANES)

    with jax.named_scope("reduce"):
        def send_image(j):
            pltpu.make_async_remote_copy(
                src_ref=istage.at[j], dst_ref=ibuf.at[me],
                send_sem=i_send, recv_sem=i_recv,
                device_id={"freq": j}, device_id_type=MESH,
            ).start()

        each_peer(me, send_image)
        ibuf[me] = istage[me]
    with jax.named_scope("wait_i"):
        most = ibuf.at[pl.ds(0, n - 1)]
        pltpu.make_async_copy(most, most, i_recv).wait()
    with jax.named_scope("last"):
        out[...] = jnp.sum(ibuf[...], axis=0)[:, : points // n]

        for c in range(CHUNKS):
            most = xbuf.at[c, pl.ds(0, n - 1)]
            pltpu.make_async_copy(most, most, x_send).wait()
            most = pbuf.at[c, pl.ds(0, n - 1)]
            pltpu.make_async_copy(most, most, p_send).wait()
        most = ibuf.at[pl.ds(0, n - 1)]
        pltpu.make_async_copy(most, most, i_send).wait()


def body(traces, freq_index, block_map, green_rec, green_src):
    n = lax.axis_size("freq")
    tsub, receivers, shots = traces.shape
    length = tsub * n
    points = green_rec.shape[3]
    fcs = 2 * freq_index.shape[0]
    per = receivers // CHUNKS
    assert freq_index.shape[0] == n == SIDE * SIDE * CORES and per == n * SUB and shots == LANES
    any_spec = pl.BlockSpec(memory_space=pl.ANY)
    vmem = pl.BlockSpec(memory_space=pltpu.VMEM)
    dma = pltpu.SemaphoreType.DMA
    out = pl.pallas_call(
        functools.partial(kernel, n),
        out_shape=jax.ShapeDtypeStruct((1, points // n), F32),
        in_specs=[any_spec, vmem, vmem, any_spec, any_spec],
        out_specs=vmem,
        scratch_shapes=[
            pltpu.VMEM((fcs, length), BF16),
            pltpu.VMEM((CHUNKS, n, tsub, SUB, LANES), BF16),
            pltpu.VMEM((SUB // 2, length, 2 * LANES), BF16),
            pltpu.VMEM((SUB, fcs, LANES), BF16),
            pltpu.VMEM((CHUNKS, n, 2, SUB, LANES), BF16),
            pltpu.VMEM((CHUNKS, n, 2, SUB, LANES), BF16),
            pltpu.VMEM((2, receivers, points), BF16),
            pltpu.VMEM((block_map.shape[0], points), F32),
            pltpu.VMEM((2, shots, points), BF16),
            pltpu.VMEM((2 * shots, points), F32),
            pltpu.VMEM((n, 1, LANES), F32),
            pltpu.VMEM((n, 1, LANES), F32),
            dma, dma((CHUNKS,)), dma, dma((CHUNKS,)), dma, dma, dma, dma,
        ],
        compiler_params=pltpu.CompilerParams(
            collective_id=0, has_side_effects=True, vmem_limit_bytes=60 * 2**20
        ),
    )(traces, freq_index[None], block_map, green_rec[0], green_src[0])
    return out[0]


def solution(mesh):
    placed = (
        P("freq", None, "groups"),
        P(),
        P(),
        P("freq", None, None, "groups"),
        P("freq", None, None, "groups"),
    )
    return jax.shard_map(
        body, mesh=mesh, in_specs=placed, out_specs=P(("groups", "freq")), check_vma=False
    )
```

time: 262 us -> 162 us (0.62)
  Pallas kernels: 0 us -> 160 us
  waiting for transfers between devices: 134 us -> 0 us
  starting transfers between devices: 44.5 us -> 0 us
  blocking collectives: 33 us -> 0 us
  local copies, waits for them, and re-layouts: 25.1 us -> 1.19 us
  between operations: 14.3 us -> 0.01 us
  matrix products: 8.12 us -> 0 us
  other arithmetic: 2.67 us -> 0 us
    pallas_call x0 -> x1, Pallas kernels: none -> 160 us  [body(): pl.pallas_call(functools.partial(kernel, n), out_shape=jax.ShapeDtypeStru...]
    all_to_all x2 -> x0, waiting for transfers between devices: 112 us -> none  [the longest x1 92.4 us: body(): lax.all_to_all(traces, FREQ, split_axis=2, concat_axis=0, tiled=True)]
    all_to_all x2 -> x0, starting transfers between devices: 44.2 us -> none  [the longest x1 27.6 us: body(): lax.all_to_all(traces, FREQ, split_axis=2, concat_axis=0, tiled=True)]
    unnamed x2 -> x0, blocking collectives: 33 us -> none
    unnamed x2 -> x0, waiting for transfers between devices: 21.5 us -> none
    unnamed x18 -> x1, local copies, waits for them, and re-layouts: 9.5 us -> 1.19 us
    dot_general x2 -> x0, matrix products: 8.12 us -> none  [the longest x1 4.68 us: back_project(): jnp.einsum('fcrx,focrs->fosx', masked, blocks, preferred_element_type=jnp...]
    convert_element_type x4 -> x0, local copies, waits for them, and re-layouts: 7.93 us -> none  [the longest x3 7.73 us: expand_map(): jnp.repeat(jnp.repeat(block_map, row_span, axis=0), col_span, axis=1)]
  transfers between devices with their start and end apart: 3 -> 0, of which waited for: 3 -> 0; matrix products, arithmetic and copies ran while one was open for 6% -> 0% of each run, Pallas kernels for 0% -> 0%
where the time goes in v2:
time: 162 us; the launch traced here: 161 us
  Pallas kernels  160 us (99%)
    pallas_call x1, Pallas kernels, body(): pl.pallas_call(functools.partial(kernel, n), out_shape=jax.ShapeDtypeStru...  160 us

profile of v2, /device:TPU:514, one launch (start us, length us, event | category | flops | bytes accessed | tf_op | source)
XLA Modules:
  0.0 161.0 jit_solution(6301423979992240203)
XLA Ops:
  0.0 159.8 %shard_map.55 = f32[1,6]{1,0:T(1,128)} custom-call(bf16[8,2048,128]{2,1,0:T(8,128)(2,1)} %traces.1, s32[1,128]{1,0:T(1,128)} %bitcast.6, s32[64,64]{1,0:T(8,128)} %block_map.1, bf16[2,2048,768]{2,1,0:T(8,128)(2,1)} %bitcast.4, bf16[2,128,768]{2,1,0:T(8,128)(2,1)} %bitcast.5), custom_call_target="tpu_custom_call" | custom-call | tf_op jit(solution)/shard_map/pallas_call | solution.py:275
  159.8 1.2 copy.7

commit v3 on v2

--- a/solution.py
+++ b/solution.py
@@ -14,9 +14,11 @@
 SUB = 8
 LANES = 128
 SIDE, CORES = 8, 2
-ORBITS = (SIDE // 2) ** 2 - 1
-STRIDE, FIRST = 11, 3
+STEPS = ((SIDE // 2) ** 2 - 1) * CORES
+MIXED = (23, 3)
+FAR_FIRST = (STEPS - 1, 23)
 BLOCK = 256
+ROOT, AIDE = 0, 1
 UNROLL = 3
 
 
@@ -39,29 +41,42 @@
     return dx, dy
 
 
-def each_peer(me, send):
-    core, y, x = me & (CORES - 1), (me // CORES) & (SIDE - 1), me // (CORES * SIDE)
-
-    def at(dx, dy, dc):
-        chip = ((x + dx) & (SIDE - 1)) * SIDE + ((y + dy) & (SIDE - 1))
-        return chip * CORES + ((core + dc) & (CORES - 1))
-
-    half = SIDE // 2
-
-    @pl.loop(0, ORBITS * CORES, unroll=UNROLL)
-    def _(i):
-        e = (i * STRIDE + FIRST) % (ORBITS * CORES)
+class Peers:
+    def __init__(self, me):
+        self.core, self.y, self.x = me & (CORES - 1), (me // CORES) & (SIDE - 1), me // (CORES * SIDE)
+
+    def at(self, dx, dy, dc):
+        chip = ((self.x + dx) & (SIDE - 1)) * SIDE + ((self.y + dy) & (SIDE - 1))
+        return chip * CORES + ((self.core + dc) & (CORES - 1))
+
+    def opposite(self, send):
+        half = SIDE // 2
+        for dx, dy in ((half, half), (half, 0), (0, half)):
+            for dc in range(CORES):
+                send(self.at(dx, dy, dc))
+
+    def turns(self, i, order, send):
+        half = SIDE // 2
+        stride, first = order
+        e = (i * stride + first) % STEPS
         k, dc = e // CORES, e & (CORES - 1)
         a, b = 1 + (k & (half - 1)), (k // half + 1) & (half - 1)
         for times in range(4):
             dx, dy = turned(a, b, times)
-            send(at(dx, dy, dc))
-
-    for dx, dy in ((half, 0), (0, half), (half, half)):
-        for dc in range(CORES):
-            send(at(dx, dy, dc))
-    for dc in range(1, CORES):
-        send(at(0, 0, dc))
+            send(self.at(dx, dy, dc))
+
+    def partner(self, send):
+        for dc in range(1, CORES):
+            send(self.at(0, 0, dc))
+
+    def each(self, order, send):
+        self.opposite(send)
+
+        @pl.loop(0, STEPS, unroll=UNROLL)
+        def _(i):
+            self.turns(i, order, send)
+
+        self.partner(send)
 
 
 def exact_dot(a, b):
@@ -69,9 +84,9 @@
 
 
 def kernel(
-    n, traces, freq_index, block_map, green_rec, green_src, out,
-    table, xbuf, xt, yb, spec, pbuf, masked, colmask, src, back, istage, ibuf,
-    x_send, x_recv, p_send, p_recv, i_send, i_recv, g_sem, s_sem,
+    n, traces, freq_hbm, map_hbm, green_rec, green_src, out,
+    freq_index, block_map, table, xbuf, xt, yb, spec, pbuf, masked, colmask, src, back, istage, ibuf,
+    x_send, x_recv, p_send, p_recv, i_send, i_recv, g_sem, s_sem, f_sem, m_sem, ready, root_in,
 ):
     me = lax.axis_index("freq")
     tsub, receivers, _ = traces.shape
@@ -84,7 +99,15 @@
     def greet(j):
         pl.semaphore_signal(barrier, inc=1, device_id={"freq": j}, device_id_type=MESH)
 
-    each_peer(me, greet)
+    peers = Peers(me)
+
+    @pl.when(me == ROOT)
+    def _():
+        greet(AIDE)
+
+    @pl.when(me != ROOT)
+    def _():
+        peers.each(FAR_FIRST, lambda j: pl.when(j > AIDE)(lambda: greet(j)))
 
     load_rec = pltpu.make_async_copy(green_rec, masked, g_sem)
     load_src = pltpu.make_async_copy(green_src, src, s_sem)
@@ -96,24 +119,76 @@
     own = [
         pltpu.make_async_copy(block_of(c, me), xbuf.at[c, me], x_recv.at[c]) for c in range(CHUNKS)
     ]
-    for copy in [*own, load_rec, load_src]:
+    small = [
+        pltpu.make_async_copy(freq_hbm, freq_index, f_sem),
+        pltpu.make_async_copy(map_hbm, block_map, m_sem),
+    ]
+    for copy in [*own, *small, load_rec, load_src]:
         copy.start()
 
+    def tell(semaphore, j):
+        pl.semaphore_signal(semaphore, inc=1, device_id={"freq": j}, device_id_type=MESH)
+
     with jax.named_scope("barrier"):
-        pl.semaphore_wait(barrier, n - 1)
+        @pl.when(me > AIDE)
+        def _():
+            pl.semaphore_wait(barrier, n - 2)
+
+        @pl.when(me == AIDE + 1)
+        def _():
+            tell(ready, AIDE)
+
+        @pl.when(me <= AIDE)
+        def _():
+            pl.semaphore_wait(ready, 1)
+
+    def send_block(c, j):
+        pltpu.make_async_remote_copy(
+            src_ref=block_of(c, j), dst_ref=xbuf.at[c, me],
+            send_sem=x_send, recv_sem=x_recv.at[c],
+            device_id={"freq": j}, device_id_type=MESH,
+        ).start()
+
+    def early(j):
+        pl.when(j != ROOT)(lambda: send_block(0, j))
+
+    def late(j):
+        pl.when(j == ROOT)(lambda: send_block(0, j))
+
+    split = STEPS // 2
+    with jax.named_scope("send_early"):
+        peers.opposite(early)
+
+        @pl.loop(0, split, unroll=UNROLL)
+        def _(i):
+            peers.turns(i, MIXED, early)
+
+    with jax.named_scope("root"):
+        @pl.when(me == AIDE)
+        def _():
+            pl.semaphore_wait(barrier, 1)
+            tell(ready, ROOT)
+            peers.each(FAR_FIRST, lambda j: pl.when(j != ROOT)(lambda: tell(root_in, j)))
+
+        @pl.when(me > AIDE)
+        def _():
+            pl.semaphore_wait(root_in, 1)
 
     with jax.named_scope("send"):
-        for c in range(CHUNKS):
-            def send_block(j, c=c):
-                pltpu.make_async_remote_copy(
-                    src_ref=block_of(c, j), dst_ref=xbuf.at[c, me],
-                    send_sem=x_send, recv_sem=x_recv.at[c],
-                    device_id={"freq": j}, device_id_type=MESH,
-                ).start()
-
-            each_peer(me, send_block)
+        peers.opposite(late)
+
+        @pl.loop(split, STEPS, unroll=UNROLL)
+        def _(i):
+            peers.turns(i - split, MIXED, late)
+            peers.turns(i, MIXED, lambda j: send_block(0, j))
+
+        peers.partner(lambda j: send_block(0, j))
+        for c in range(1, CHUNKS):
+            peers.each(MIXED, lambda j, c=c: send_block(c, j))
 
     with jax.named_scope("table"):
+        for copy in small:
+            copy.wait()
         freqs = freq_index.shape[1]
         diagonal = iota((freqs, freqs), 0) == iota((freqs, freqs), 1)
         column = jnp.sum(
@@ -197,7 +272,7 @@
                     device_id={"freq": j}, device_id_type=MESH,
                 ).start()
 
-            each_peer(me, send_spectrum)
+            peers.each(MIXED, send_spectrum)
             pbuf[c, me] = spec[c, me]
 
     def project(c):
@@ -244,7 +319,7 @@
                 device_id={"freq": j}, device_id_type=MESH,
             ).start()
 
-        each_peer(me, send_image)
+        peers.each(FAR_FIRST, send_image)
         ibuf[me] = istage[me]
     with jax.named_scope("wait_i"):
         most = ibuf.at[pl.ds(0, n - 1)]
@@ -275,9 +350,11 @@
     out = pl.pallas_call(
         functools.partial(kernel, n),
         out_shape=jax.ShapeDtypeStruct((1, points // n), F32),
-        in_specs=[any_spec, vmem, vmem, any_spec, any_spec],
+        in_specs=[any_spec] * 5,
         out_specs=vmem,
         scratch_shapes=[
+            pltpu.VMEM((1, n), jnp.int32),
+            pltpu.VMEM(block_map.shape, jnp.int32),
             pltpu.VMEM((fcs, length), BF16),
             pltpu.VMEM((CHUNKS, n, tsub, SUB, LANES), BF16),
             pltpu.VMEM((SUB // 2, length, 2 * LANES), BF16),
@@ -290,7 +367,8 @@
             pltpu.VMEM((2 * shots, points), F32),
             pltpu.VMEM((n, 1, LANES), F32),
             pltpu.VMEM((n, 1, LANES), F32),
-            dma, dma((CHUNKS,)), dma, dma((CHUNKS,)), dma, dma, dma, dma,
+            dma, dma((CHUNKS,)), dma, dma((CHUNKS,)), dma, dma, dma, dma, dma, dma,
+            pltpu.SemaphoreType.REGULAR, pltpu.SemaphoreType.REGULAR,
         ],
         compiler_params=pltpu.CompilerParams(
             collective_id=0, has_side_effects=True, vmem_limit_bytes=60 * 2**20

time: 162 us -> 156 us (0.963)
  Pallas kernels: 160 us -> 153 us
    pallas_call x1, Pallas kernels: 160 us -> 153 us  [body(): pl.pallas_call(functools.partial(kernel, n), out_shape=jax.ShapeDtypeStru...]
where the time goes in v3:
time: 156 us; the launch traced here: 154 us
  Pallas kernels  153 us (98%)
    pallas_call x1, Pallas kernels, body(): pl.pallas_call(functools.partial(kernel, n), out_shape=jax.ShapeDtypeStru...  153 us

profile of v3, /device:TPU:514, one launch (start us, length us, event | category | flops | bytes accessed | tf_op | source)
XLA Modules:
  0.0 154.2 jit_solution(1077565302891159924)
XLA Ops:
  0.0 153.0 %shard_map.55 = f32[1,6]{1,0:T(1,128)} custom-call(bf16[8,2048,128]{2,1,0:T(8,128)(2,1)} %traces.1, s32[1,128]{1,0:T(1,128)} %bitcast.6, s32[64,64]{1,0:T(8,128)} %map_hbm.1, bf16[2,2048,768]{2,1,0:T(8,128)(2,1)} %bitcast.4, bf16[2,128,768]{2,1,0:T(8,128)(2,1)} %bitcast.5), custom_call_target="tpu_custom_call" | custom-call | tf_op jit(solution)/shard_map/pallas_call | solution.py:350
  153.0 1.2 copy.7

commit v4 on v3

--- a/solution.py
+++ b/solution.py
@@ -15,7 +15,7 @@
 LANES = 128
 SIDE, CORES = 8, 2
 STEPS = ((SIDE // 2) ** 2 - 1) * CORES
-MIXED = (23, 3)
+MIXED = ((17, 8), (19, 23))
 FAR_FIRST = (STEPS - 1, 23)
 BLOCK = 256
 ROOT, AIDE = 0, 1
@@ -79,13 +79,17 @@
         self.partner(send)
 
 
-def exact_dot(a, b):
-    return jnp.dot(a, b, preferred_element_type=F32, precision=lax.Precision.HIGHEST)
+def three_parts(a):
+    parts = []
+    for _ in range(3):
+        parts.append(a.astype(BF16))
+        a = a - parts[-1].astype(F32)
+    return parts
 
 
 def kernel(
     n, traces, freq_hbm, map_hbm, green_rec, green_src, out,
-    freq_index, block_map, table, xbuf, xt, yb, spec, pbuf, masked, colmask, src, back, istage, ibuf,
+    freq_index, block_map, table, xbuf, xt, yb, spec, pbuf, masked, colmask, src, back, pick, fold, istage, ibuf,
     x_send, x_recv, p_send, p_recv, i_send, i_recv, g_sem, s_sem, f_sem, m_sem, ready, root_in,
 ):
     me = lax.axis_index("freq")
@@ -161,7 +165,7 @@
 
         @pl.loop(0, split, unroll=UNROLL)
         def _(i):
-            peers.turns(i, MIXED, early)
+            peers.turns(i, MIXED[0], early)
 
     with jax.named_scope("root"):
         @pl.when(me == AIDE)
@@ -179,12 +183,12 @@
 
         @pl.loop(split, STEPS, unroll=UNROLL)
         def _(i):
-            peers.turns(i - split, MIXED, late)
-            peers.turns(i, MIXED, lambda j: send_block(0, j))
+            peers.turns(i - split, MIXED[0], late)
+            peers.turns(i, MIXED[0], lambda j: send_block(0, j))
 
         peers.partner(lambda j: send_block(0, j))
         for c in range(1, CHUNKS):
-            peers.each(MIXED, lambda j, c=c: send_block(c, j))
+            peers.each(MIXED[c], lambda j, c=c: send_block(c, j))
 
     with jax.named_scope("table"):
         for copy in small:
@@ -222,6 +226,9 @@
         BLOCK, lambda row: row % SUB * tb + row // SUB % 2 * fb + row // (2 * SUB)
     )
     scale = 1.0 / math.sqrt(length)
+    each = points // n
+    pick[...] = one_hot(iota((n, points), 1) // each == iota((n, points), 0)).astype(BF16)
+    fold[...] = one_hot(iota((points, LANES), 0) % each == iota((points, LANES), 1)).astype(BF16)
     back[...] = jnp.zeros_like(back)
 
     def transform(c):
@@ -272,7 +279,7 @@
                     device_id={"freq": j}, device_id_type=MESH,
                 ).start()
 
-            peers.each(MIXED, send_spectrum)
+            peers.each(MIXED[0], send_spectrum)
             pbuf[c, me] = spec[c, me]
 
     def project(c):
@@ -306,10 +313,9 @@
             image += jnp.sum(
                 src[o].astype(F32) * back[o * shots : (o + 1) * shots, :], axis=0, keepdims=True
             )
-        each = points // n
-        mine = one_hot(iota((n, points), 1) // each == iota((n, points), 0)) * image
-        fold = one_hot(iota((points, LANES), 0) % each == iota((points, LANES), 1))
-        istage[...] = exact_dot(mine, fold).reshape(n, 1, LANES)
+        rows = jnp.concatenate([pick[...] * p for p in three_parts(image)], axis=0)
+        folded = jnp.dot(rows, fold[...], preferred_element_type=F32).reshape(3, n, LANES)
+        istage[...] = (folded[0] + (folded[1] + folded[2])).reshape(n, 1, LANES)
 
     with jax.named_scope("reduce"):
         def send_image(j):
@@ -365,6 +371,8 @@
             pltpu.VMEM((block_map.shape[0], points), F32),
             pltpu.VMEM((2, shots, points), BF16),
             pltpu.VMEM((2 * shots, points), F32),
+            pltpu.VMEM((n, points), BF16),
+            pltpu.VMEM((points, LANES), BF16),
             pltpu.VMEM((n, 1, LANES), F32),
             pltpu.VMEM((n, 1, LANES), F32),
             dma, dma((CHUNKS,)), dma, dma((CHUNKS,)), dma, dma, dma, dma, dma, dma,

time: 156 us -> 149 us (0.955)
  Pallas kernels: 153 us -> 146 us
    pallas_call x1, Pallas kernels: 153 us -> 146 us  [body(): pl.pallas_call(functools.partial(kernel, n), out_shape=jax.ShapeDtypeStru...]
where the time goes in v4:
time: 149 us; the launch traced here: 147 us
  Pallas kernels  146 us (98%)
    pallas_call x1, Pallas kernels, body(): pl.pallas_call(functools.partial(kernel, n), out_shape=jax.ShapeDtypeStru...  146 us

profile of v4, /device:TPU:514, one launch (start us, length us, event | category | flops | bytes accessed | tf_op | source)
XLA Modules:
  0.0 147.4 jit_solution(5076590373413938306)
XLA Ops:
  0.0 146.2 %shard_map.55 = f32[1,6]{1,0:T(1,128)} custom-call(bf16[8,2048,128]{2,1,0:T(8,128)(2,1)} %traces.1, s32[1,128]{1,0:T(1,128)} %bitcast.6, s32[64,64]{1,0:T(8,128)} %map_hbm.1, bf16[2,2048,768]{2,1,0:T(8,128)(2,1)} %bitcast.4, bf16[2,128,768]{2,1,0:T(8,128)(2,1)} %bitcast.5), custom_call_target="tpu_custom_call" | custom-call | tf_op jit(solution)/shard_map/pallas_call | solution.py:356
  146.2 1.2 copy.7

commit v5 on v4

--- a/solution.py
+++ b/solution.py
@@ -159,7 +159,7 @@
     def late(j):
         pl.when(j == ROOT)(lambda: send_block(0, j))
 
-    split = STEPS // 2
+    split = STEPS * 2 // 5
     with jax.named_scope("send_early"):
         peers.opposite(early)
 
@@ -181,9 +181,12 @@
     with jax.named_scope("send"):
         peers.opposite(late)
 
+        @pl.loop(0, split)
+        def _(i):
+            peers.turns(i, MIXED[0], late)
+
         @pl.loop(split, STEPS, unroll=UNROLL)
         def _(i):
-            peers.turns(i - split, MIXED[0], late)
             peers.turns(i, MIXED[0], lambda j: send_block(0, j))
 
         peers.partner(lambda j: send_block(0, j))

time: 149 us -> 149 us (level)
  no operation moved by 1% of the time
where the time goes in v5:
time: 149 us; the launch traced here: 148 us
  Pallas kernels  146 us (98%)
    pallas_call x1, Pallas kernels, body(): pl.pallas_call(functools.partial(kernel, n), out_shape=jax.ShapeDtypeStru...  146 us

profile of v5, /device:TPU:514, one launch (start us, length us, event | category | flops | bytes accessed | tf_op | source)
XLA Modules:
  0.0 147.6 jit_solution(13379642125161687141)
XLA Ops:
  0.0 146.4 %shard_map.55 = f32[1,6]{1,0:T(1,128)} custom-call(bf16[8,2048,128]{2,1,0:T(8,128)(2,1)} %traces.1, s32[1,128]{1,0:T(1,128)} %bitcast.6, s32[64,64]{1,0:T(8,128)} %map_hbm.1, bf16[2,2048,768]{2,1,0:T(8,128)(2,1)} %bitcast.4, bf16[2,128,768]{2,1,0:T(8,128)(2,1)} %bitcast.5), custom_call_target="tpu_custom_call" | custom-call | tf_op jit(solution)/shard_map/pallas_call | solution.py:359
  146.4 1.2 copy.7
